TPU v7x, 768 devices: a whole 4x8x12 slice. The times are simulated.
768 devices in a mesh: curve: 96 (over y, z), seg: 8 (over x, core).
Axes of the slice: x: 4, y: 8, z: 12, core: 2. Of those that a mesh axis runs over, the one named last changes fastest.
Arguments:
- solution: bfloat16 [393216, 128], P(('curve', 'seg')), may hold values from -6 to 6
- viscosity: float32 [3145728], P(('curve', 'seg')), may hold values from 0.1 to 10
- slot_index: int32 [3145728, 4], P(('curve', 'seg')), may hold values from 0 to 1279, as said below
- slot_weight: int32 [3145728, 4], P(('curve', 'seg')), may hold values from -1 to 8, as said below
- mirror_rows: int32 [768, 4, 192], P(('curve', 'seg')), may hold values from 0 to 511
- ghost_live: int32 [768, 4], P(('curve', 'seg')), may hold values from 0 to 192, as said below
- cell_count: int32 [768], P(('curve', 'seg')), may hold values from 512 to 4096, as said below
- viscous_block: bfloat16 [128, 128], replicated, may hold values from -0.5 to 0.5
- pressure_block: bfloat16 [128, 128], replicated, may hold values from -0.5 to 0.5
Outputs:
- residual: float32 [393216, 128], P(('curve', 'seg'))
Inputs may be any that keep to these rules, and one draw needn't show every extreme that they name: `slot_index`: column 0 of each element is one of its device's owned blocks; other columns point to owned blocks or to ghost entries; ghost entries past a list's live count read zeros. `slot_weight`: each entry is one of -1, 3, 6, 8; column 0 is 8. `ghost_live`: some list is full in every draw. `cell_count`: some device is full in every draw; loads are skewed.
All inputs are finite; a program needn't handle non-finite values.
Results may differ from a plain program's by a relative error of at most 0.0035.
Values may be sent and summed in bfloat16 or wider, within the bound.
A program may use at most 32 MiB of HBM per device.

v0:
```python
import jax
import jax.numpy as jnp
from jax import lax
from jax.sharding import PartitionSpec as P


def shifted(block, axis, distance):
    devices = range(lax.axis_size(axis))
    route = [(i - distance, i) for i in devices if i - distance in devices]
    return lax.ppermute(block, axis, route)


def shift_list(region_count):
    return [(region // 2 + 1) * (1 if region % 2 == 0 else -1) for region in range(region_count)]


def split_parts(values):
    upper = values.astype(jnp.bfloat16)
    lower = (values - upper.astype(jnp.float32)).astype(jnp.bfloat16)
    return (upper, lower)


def transposed_product(table, values):
    upper, lower = split_parts(values)
    first = jnp.einsum("er,ec->rc", table, upper, preferred_element_type=jnp.float32)
    return first + jnp.einsum("er,ec->rc", table, lower, preferred_element_type=jnp.float32)


def weight_table(indices, block_weights, column_total):
    columns = jnp.arange(column_total, dtype=jnp.int32)
    table = jnp.zeros((indices.shape[0], column_total), jnp.float32)
    for slot_pos in range(indices.shape[1]):
        hit = indices[:, slot_pos, None] == columns[None, :]
        table = table + jnp.where(hit, block_weights[:, slot_pos, None], 0.0)
    return table.astype(jnp.bfloat16)


def per_device(
    solution,
    viscosity,
    slot_index,
    slot_weight,
    mirror_rows,
    ghost_live,
    cell_count,
    viscous_block,
    pressure_block,
):
    owned_rows = solution.shape[0]
    width = solution.shape[1]
    region_count = mirror_rows.shape[1]
    ghost_rows = mirror_rows.shape[2]
    slot_total = slot_index.shape[1]
    column_total = owned_rows + region_count * ghost_rows
    offsets = shift_list(region_count)
    ghost_pos = jnp.arange(ghost_rows, dtype=jnp.int32)
    elem_rows = viscosity.shape[0]
    block_rows = min(1024, elem_rows)
    block_total = elem_rows // block_rows
    live = (jnp.arange(elem_rows, dtype=jnp.int32) < cell_count[0]).astype(jnp.float32)
    weights = slot_weight.astype(jnp.float32) / 8.0 * live[:, None]
    index_blocks = slot_index.reshape(block_total, block_rows, slot_total)
    weight_blocks = weights.reshape(block_total, block_rows, slot_total)
    visc_blocks = viscosity.reshape(block_total, block_rows)
    owned_columns = jnp.arange(owned_rows, dtype=jnp.int32)
    list_mask = ghost_pos[None, :] < ghost_live[0][:, None]
    mirror_hit = (mirror_rows[0][:, :, None] == owned_columns[None, None, :]) & list_mask[
        :, :, None
    ]
    mirror_table = mirror_hit.reshape(region_count * ghost_rows, owned_rows).astype(jnp.bfloat16)
    outgoing_all = jnp.dot(mirror_table, solution, preferred_element_type=jnp.float32).astype(
        jnp.bfloat16
    )
    outgoing = [
        outgoing_all[region * ghost_rows : (region + 1) * ghost_rows]
        for region in range(region_count)
    ]
    incoming = [None] * region_count
    for region in range(region_count):
        incoming[region] = shifted(outgoing[region], ("curve", "seg"), offsets[region])

    def apply_matrices(element_in, local_visc):
        element_out = local_visc[:, None] * jnp.dot(
            element_in, viscous_block, preferred_element_type=jnp.float32
        )
        return element_out + jnp.dot(element_in, pressure_block, preferred_element_type=jnp.float32)

    start_partial = jnp.zeros((column_total, width), jnp.float32)
    ghost_stack = jnp.concatenate(incoming, axis=0)
    extended = jnp.concatenate([solution, ghost_stack], axis=0)

    def element_block(partial_value, inputs):
        indices, block_weights, local_visc = inputs
        table = weight_table(indices, block_weights, column_total)
        element_in = jnp.dot(table, extended, preferred_element_type=jnp.float32)
        element_out = apply_matrices(element_in.astype(jnp.bfloat16), local_visc)
        return (partial_value + transposed_product(table, element_out), None)

    partial_value, unused = lax.scan(
        element_block, start_partial, (index_blocks, weight_blocks, visc_blocks)
    )
    ghost_part = partial_value[owned_rows:].reshape(region_count, ghost_rows, width)
    returned = [None] * region_count
    for region in range(region_count):
        returned[region] = shifted(ghost_part[region], ("curve", "seg"), -offsets[region])
    returned_all = jnp.concatenate(returned, axis=0)
    return partial_value[:owned_rows] + transposed_product(mirror_table, returned_all)


def solution(mesh):
    return jax.shard_map(
        per_device,
        mesh=mesh,
        in_specs=(
            P(("curve", "seg"), None),
            P(("curve", "seg")),
            P(("curve", "seg"), None),
            P(("curve", "seg"), None),
            P(("curve", "seg"), None, None),
            P(("curve", "seg"), None),
            P(("curve", "seg")),
            P(),
            P(),
        ),
        out_specs=P(("curve", "seg"), None),
        check_vma=False,
    )
```

profile of v0, /device:TPU:32, one launch (start us, length us, event | category | flops | bytes accessed | tf_op | source)
XLA Modules:
  0.0 107.3 jit_solution(16153732100141251545)
XLA Ops:
  0.0 0.7 iota_compare_fusion.6
  0.8 0.8 eq.76
  1.6 1.4 %fusion.11 = bf16[768,128]{1,0:T(8,128)(2,1)S(1)} fusion(bf16[512,128]{1,0:T(8,128)(2,1)} %param.11, s32[768]{0:T(1024)S(1)} %eq.76, pred[768]{0:T(1024)(128)(4,1)S(1)} %lt.41), kind=kOutput, calls=%fused_computation.22 | convolution fusion | flops 101548032 | bytes 331520 | tf_op jit(solution)/shard_map/dot_general | solution.py:71
  3.1 16.7 %collective-permute-start.3 = (bf16[192,128]{1,0:T(8,128)(2,1)S(1)}, bf16[192,128]{1,0:T(8,128)(2,1)S(1)}, u32[]{:S(2)}, u32[]{:S(2)}) collective-permute-start(bf16[192,128]{1,0:T(8,128)(2,1)S(1)} %get-tuple-element.103), channel_id=1, source_target_pairs={{2,0},{3,1},{4,2},{5,3},{6,4},{7,5},{8,6},{9,7},{10,8},{11,9},{12,... | collective-permute-start | bytes 147464 | tf_op jit(solution)/shard_map/ppermute | solution.py:10
  19.8 1.9 %collective-permute-start.2 = (bf16[192,128]{1,0:T(8,128)(2,1)S(1)}, bf16[192,128]{1,0:T(8,128)(2,1)S(1)}, u32[]{:S(2)}, u32[]{:S(2)}) collective-permute-start(bf16[192,128]{1,0:T(8,128)(2,1)S(1)} %get-tuple-element.104), channel_id=1, source_target_pairs={{0,2},{1,3},{2,4},{3,5},{4,6},{5,7},{6,8},{7,9},{8,10},{9,11},{10,... | collective-permute-start | bytes 147464 | tf_op jit(solution)/shard_map/ppermute | solution.py:10
  21.7 8.2 %collective-permute-start.1 = (bf16[192,128]{1,0:T(8,128)(2,1)S(1)}, bf16[192,128]{1,0:T(8,128)(2,1)S(1)}, u32[]{:S(2)}, u32[]{:S(2)}) collective-permute-start(bf16[192,128]{1,0:T(8,128)(2,1)S(1)} %get-tuple-element.105), channel_id=1, source_target_pairs={{1,0},{2,1},{3,2},{4,3},{5,4},{6,5},{7,6},{8,7},{9,8},{10,9},{11,1... | collective-permute-start | bytes 147464 | tf_op jit(solution)/shard_map/ppermute | solution.py:10
  29.9 1.9 %collective-permute-start = (bf16[192,128]{1,0:T(8,128)(2,1)S(1)}, bf16[192,128]{1,0:T(8,128)(2,1)S(1)}, u32[]{:S(2)}, u32[]{:S(2)}) collective-permute-start(bf16[192,128]{1,0:T(8,128)(2,1)S(1)} %get-tuple-element.106), channel_id=1, source_target_pairs={{0,1},{1,2},{2,3},{3,4},{4,5},{5,6},{6,7},{7,8},{8,9},{9,10},{10,1... | collective-permute-start | bytes 147464 | tf_op jit(solution)/shard_map/ppermute | solution.py:10
  32.6 8.1 %collective-permute-done = bf16[192,128]{1,0:T(8,128)(2,1)S(1)} collective-permute-done((bf16[192,128]{1,0:T(8,128)(2,1)S(1)}, bf16[192,128]{1,0:T(8,128)(2,1)S(1)}, u32[]{:S(2)}, u32[]{:S(2)}) %collective-permute-start) | collective-permute-done | bytes 49184 | tf_op jit(solution)/shard_map/ppermute | solution.py:10
  40.9 46.4 %while.11 = (s32[]{:T(128)}, f32[1280,128]{1,0:T(8,128)S(1)}, s32[4,1024,4]{1,2,0:T(4,128)}, f32[4,1024,4]{1,2,0:T(4,128)S(1)}, f32[4,1024]{1,0:T(4,128)S(1)}, /...) while((s32[]{:T(128)}, f32[1280,128]{1,0:T(8,128)S(1)}, ...), condition=%wide.region_1.2_spmd.clone, body=%wide.region_0.1_spmd.clone.sunk | while | flops 1122467840 | bytes 6664323 | solution.py:99
  41.0 0.7 dynamic-slice_bitcast_fusion.5
  41.7 3.6 %convolution_convert_fusion.2 = bf16[1024,128]{1,0:T(8,128)(2,1)S(1)} fusion(bf16[1280,128]{1,0:T(8,128)(2,1)S(1)} %get-tuple-element.197, f32[1024]{0:T(1024)S(1)} %bitcast.62, s32[1024]{0:T(1024)S(1)} %bitcast.74, f32[1024]{0:T(1024)S(1)} %bitcast.65, s32[1024]{0:T(1024)S(1)} %bitcast.77, f32[1024]{0:T(1024)S(1)} %bitcast.68, ...), kind=kOutput, calls=%fused_computation.9.clone.1 | convolution fusion | flops 351404032 | bytes 622592 | tf_op jit(solution)/shard_map/while/body/eval_jaxpr/dot_general | solution.py:95
  45.8 3.1 %fusion.58 = f32[1280,128]{1,0:T(8,128)S(1)} fusion(f32[1024,128]{1,0:T(8,128)S(1)} %convolution_add_fusion.3, f32[1024]{0:T(1024)S(1)} %bitcast.63, s32[1024]{0:T(1024)S(1)} %bitcast.75, f32[1024]{0:T(1024)S(1)} %bitcast.66, s32[1024]{0:T(1024)S(1)} %bitcast.78, f32[1024]{0:T(1024)S(1)} %bitcast.69, s32[1024]{0:T(1024)S(1)} %bitcast.81, ...), kind=kOutput, calls=%fused_computation.12.clone.1 | convolution fusion | flops 351404032 | bytes 1212416 | tf_op jit(solution)/shard_map/while/body/eval_jaxpr/er,ec->rc/dot_general | solution.py:25
  48.9 3.6 %fusion.59 = f32[1280,128]{1,0:T(8,128)S(1)} fusion(f32[1280,128]{1,0:T(8,128)S(1)} %fusion.58, f32[1280,128]{1,0:T(8,128)S(1)} %get-tuple-element.183, pred[]{:T(512)S(6)} %compare.3, f32[1024,128]{1,0:T(8,128)S(1)} %convolution_add_fusion.3, f32[1024]{0:T(1024)S(1)} %bitcast.64, s32[1024]{0:T(1024)S(1)} %bitcast.76, f32[1024]{0:T(1024)S(1)} %bitcast.67, ...), kind=kOutput, calls=%fused_computation.6.clone.1 | convolution fusion | flops 352288768 | bytes 2523137 | tf_op jit(solution)/shard_map/while/body/eval_jaxpr/er,ec->rc/dot_general | solution.py:26
  52.6 0.7 dynamic-slice_bitcast_fusion.5
  53.3 3.6 %convolution_convert_fusion.2 = bf16[1024,128]{1,0:T(8,128)(2,1)S(1)} fusion(bf16[1280,128]{1,0:T(8,128)(2,1)S(1)} %get-tuple-element.197, f32[1024]{0:T(1024)S(1)} %bitcast.62, s32[1024]{0:T(1024)S(1)} %bitcast.74, f32[1024]{0:T(1024)S(1)} %bitcast.65, s32[1024]{0:T(1024)S(1)} %bitcast.77, f32[1024]{0:T(1024)S(1)} %bitcast.68, ...), kind=kOutput, calls=%fused_computation.9.clone.1 | convolution fusion | flops 351404032 | bytes 622592 | tf_op jit(solution)/shard_map/while/body/eval_jaxpr/dot_general | solution.py:95
  57.4 3.1 %fusion.58 = f32[1280,128]{1,0:T(8,128)S(1)} fusion(f32[1024,128]{1,0:T(8,128)S(1)} %convolution_add_fusion.3, f32[1024]{0:T(1024)S(1)} %bitcast.63, s32[1024]{0:T(1024)S(1)} %bitcast.75, f32[1024]{0:T(1024)S(1)} %bitcast.66, s32[1024]{0:T(1024)S(1)} %bitcast.78, f32[1024]{0:T(1024)S(1)} %bitcast.69, s32[1024]{0:T(1024)S(1)} %bitcast.81, ...), kind=kOutput, calls=%fused_computation.12.clone.1 | convolution fusion | flops 351404032 | bytes 1212416 | tf_op jit(solution)/shard_map/while/body/eval_jaxpr/er,ec->rc/dot_general | solution.py:25
  60.5 3.6 %fusion.59 = f32[1280,128]{1,0:T(8,128)S(1)} fusion(f32[1280,128]{1,0:T(8,128)S(1)} %fusion.58, f32[1280,128]{1,0:T(8,128)S(1)} %get-tuple-element.183, pred[]{:T(512)S(6)} %compare.3, f32[1024,128]{1,0:T(8,128)S(1)} %convolution_add_fusion.3, f32[1024]{0:T(1024)S(1)} %bitcast.64, s32[1024]{0:T(1024)S(1)} %bitcast.76, f32[1024]{0:T(1024)S(1)} %bitcast.67, ...), kind=kOutput, calls=%fused_computation.6.clone.1 | convolution fusion | flops 352288768 | bytes 2523137 | tf_op jit(solution)/shard_map/while/body/eval_jaxpr/er,ec->rc/dot_general | solution.py:26
  64.2 0.7 dynamic-slice_bitcast_fusion.5
  64.9 3.6 %convolution_convert_fusion.2 = bf16[1024,128]{1,0:T(8,128)(2,1)S(1)} fusion(bf16[1280,128]{1,0:T(8,128)(2,1)S(1)} %get-tuple-element.197, f32[1024]{0:T(1024)S(1)} %bitcast.62, s32[1024]{0:T(1024)S(1)} %bitcast.74, f32[1024]{0:T(1024)S(1)} %bitcast.65, s32[1024]{0:T(1024)S(1)} %bitcast.77, f32[1024]{0:T(1024)S(1)} %bitcast.68, ...), kind=kOutput, calls=%fused_computation.9.clone.1 | convolution fusion | flops 351404032 | bytes 622592 | tf_op jit(solution)/shard_map/while/body/eval_jaxpr/dot_general | solution.py:95
  69.0 3.1 %fusion.58 = f32[1280,128]{1,0:T(8,128)S(1)} fusion(f32[1024,128]{1,0:T(8,128)S(1)} %convolution_add_fusion.3, f32[1024]{0:T(1024)S(1)} %bitcast.63, s32[1024]{0:T(1024)S(1)} %bitcast.75, f32[1024]{0:T(1024)S(1)} %bitcast.66, s32[1024]{0:T(1024)S(1)} %bitcast.78, f32[1024]{0:T(1024)S(1)} %bitcast.69, s32[1024]{0:T(1024)S(1)} %bitcast.81, ...), kind=kOutput, calls=%fused_computation.12.clone.1 | convolution fusion | flops 351404032 | bytes 1212416 | tf_op jit(solution)/shard_map/while/body/eval_jaxpr/er,ec->rc/dot_general | solution.py:25
  72.1 3.6 %fusion.59 = f32[1280,128]{1,0:T(8,128)S(1)} fusion(f32[1280,128]{1,0:T(8,128)S(1)} %fusion.58, f32[1280,128]{1,0:T(8,128)S(1)} %get-tuple-element.183, pred[]{:T(512)S(6)} %compare.3, f32[1024,128]{1,0:T(8,128)S(1)} %convolution_add_fusion.3, f32[1024]{0:T(1024)S(1)} %bitcast.64, s32[1024]{0:T(1024)S(1)} %bitcast.76, f32[1024]{0:T(1024)S(1)} %bitcast.67, ...), kind=kOutput, calls=%fused_computation.6.clone.1 | convolution fusion | flops 352288768 | bytes 2523137 | tf_op jit(solution)/shard_map/while/body/eval_jaxpr/er,ec->rc/dot_general | solution.py:26
  75.8 0.7 dynamic-slice_bitcast_fusion.5
  76.5 3.6 %convolution_convert_fusion.2 = bf16[1024,128]{1,0:T(8,128)(2,1)S(1)} fusion(bf16[1280,128]{1,0:T(8,128)(2,1)S(1)} %get-tuple-element.197, f32[1024]{0:T(1024)S(1)} %bitcast.62, s32[1024]{0:T(1024)S(1)} %bitcast.74, f32[1024]{0:T(1024)S(1)} %bitcast.65, s32[1024]{0:T(1024)S(1)} %bitcast.77, f32[1024]{0:T(1024)S(1)} %bitcast.68, ...), kind=kOutput, calls=%fused_computation.9.clone.1 | convolution fusion | flops 351404032 | bytes 622592 | tf_op jit(solution)/shard_map/while/body/eval_jaxpr/dot_general | solution.py:95
  80.6 3.1 %fusion.58 = f32[1280,128]{1,0:T(8,128)S(1)} fusion(f32[1024,128]{1,0:T(8,128)S(1)} %convolution_add_fusion.3, f32[1024]{0:T(1024)S(1)} %bitcast.63, s32[1024]{0:T(1024)S(1)} %bitcast.75, f32[1024]{0:T(1024)S(1)} %bitcast.66, s32[1024]{0:T(1024)S(1)} %bitcast.78, f32[1024]{0:T(1024)S(1)} %bitcast.69, s32[1024]{0:T(1024)S(1)} %bitcast.81, ...), kind=kOutput, calls=%fused_computation.12.clone.1 | convolution fusion | flops 351404032 | bytes 1212416 | tf_op jit(solution)/shard_map/while/body/eval_jaxpr/er,ec->rc/dot_general | solution.py:25
  83.7 3.6 %fusion.59 = f32[1280,128]{1,0:T(8,128)S(1)} fusion(f32[1280,128]{1,0:T(8,128)S(1)} %fusion.58, f32[1280,128]{1,0:T(8,128)S(1)} %get-tuple-element.183, pred[]{:T(512)S(6)} %compare.3, f32[1024,128]{1,0:T(8,128)S(1)} %convolution_add_fusion.3, f32[1024]{0:T(1024)S(1)} %bitcast.64, s32[1024]{0:T(1024)S(1)} %bitcast.76, f32[1024]{0:T(1024)S(1)} %bitcast.67, ...), kind=kOutput, calls=%fused_computation.6.clone.1 | convolution fusion | flops 352288768 | bytes 2523137 | tf_op jit(solution)/shard_map/while/body/eval_jaxpr/er,ec->rc/dot_general | solution.py:26
  87.4 1.9 %collective-permute-start.4 = (f32[192,128]{1,0:T(8,128)S(1)}, f32[192,128]{1,0:T(8,128)S(1)}, u32[]{:S(2)}, u32[]{:S(2)}) collective-permute-start(f32[192,128]{1,0:T(8,128)S(1)} %get-tuple-element.101), channel_id=1, source_target_pairs={{1,0},{2,1},{3,2},{4,3},{5,4},{6,5},{7,6},{8,7},{9,8},{10,9},{11,1... | collective-permute-start | bytes 294920 | tf_op jit(solution)/shard_map/ppermute | solution.py:10
  89.3 1.9 %collective-permute-start.7 = (f32[192,128]{1,0:T(8,128)S(1)}, f32[192,128]{1,0:T(8,128)S(1)}, u32[]{:S(2)}, u32[]{:S(2)}) collective-permute-start(f32[192,128]{1,0:T(8,128)S(1)} %get-tuple-element.99), channel_id=1, source_target_pairs={{0,2},{1,3},{2,4},{3,5},{4,6},{5,7},{6,8},{7,9},{8,10},{9,11},{10,... | collective-permute-start | bytes 294920 | tf_op jit(solution)/shard_map/ppermute | solution.py:10
  91.2 2.4 %collective-permute-start.5 = (f32[192,128]{1,0:T(8,128)S(1)}, f32[192,128]{1,0:T(8,128)S(1)}, u32[]{:S(2)}, u32[]{:S(2)}) collective-permute-start(f32[192,128]{1,0:T(8,128)S(1)} %get-tuple-element.100), channel_id=1, source_target_pairs={{0,1},{1,2},{2,3},{3,4},{4,5},{5,6},{6,7},{7,8},{8,9},{9,10},{10,1... | collective-permute-start | bytes 294920 | tf_op jit(solution)/shard_map/ppermute | solution.py:10
  93.6 9.1 %collective-permute-start.6 = (f32[192,128]{1,0:T(8,128)S(1)}, f32[192,128]{1,0:T(8,128)S(1)}, u32[]{:S(2)}, u32[]{:S(2)}) collective-permute-start(f32[192,128]{1,0:T(8,128)S(1)} %get-tuple-element.102), channel_id=1, source_target_pairs={{2,0},{3,1},{4,2},{5,3},{6,4},{7,5},{8,6},{9,7},{10,8},{11,9},{12,... | collective-permute-start | bytes 294920 | tf_op jit(solution)/shard_map/ppermute | solution.py:10
  102.9 2.0 %collective-permute-done.6 = f32[192,128]{1,0:T(8,128)S(1)} collective-permute-done((f32[192,128]{1,0:T(8,128)S(1)}, f32[192,128]{1,0:T(8,128)S(1)}, u32[]{:S(2)}, u32[]{:S(2)}) %collective-permute-start.6) | collective-permute-done | bytes 98336 | tf_op jit(solution)/shard_map/ppermute | solution.py:10
  105.0 0.8 fusion.5
  105.8 1.5 %slice_add_fusion = f32[512,128]{1,0:T(8,128)} fusion(f32[1280,128]{1,0:T(8,128)S(1)} %get-tuple-element.47, f32[512,128]{1,0:T(8,128)S(1)} %fusion.5, f32[768,128]{1,0:T(8,128)S(1)} %constant_dynamic-update-slice_fusion.5, s32[768]{0:T(1024)S(1)} %eq.76, pred[768]{0:T(1024)(128)(4,1)S(1)} %lt.41), kind=kOutput, calls=%fused_computation.31 | convolution fusion | flops 101679104 | bytes 1183488 | tf_op jit(solution)/shard_map/er,ec->rc/dot_general | solution.py:25
  (56 shorter events, 2.4 us)
Async XLA Ops:
  1.6 30.9 %copy-start.3 = (s32[4096,4]{0,1:T(4,128)S(1)}, s32[4096,4]{0,1:T(4,128)}, u32[]{:S(2)}) copy-start(s32[4096,4]{0,1:T(4,128)} %param.14) | copy-start | bytes 196612
  1.6 31.0 %copy-start.2 = (bf16[512,128]{1,0:T(8,128)(2,1)S(1)}, bf16[512,128]{1,0:T(8,128)(2,1)}, u32[]{:S(2)}) copy-start(bf16[512,128]{1,0:T(8,128)(2,1)} %param.11) | copy-start | bytes 393220
  3.0 29.6 %copy-start.4 = (f32[4096]{0:T(1024)S(1)}, f32[4096]{0:T(1024)}, u32[]{:S(2)}) copy-start(f32[4096]{0:T(1024)} %param.12) | copy-start | bytes 49156
  3.0 37.8 %copy-start = (bf16[128,128]{1,0:T(8,128)(2,1)S(1)}, bf16[128,128]{1,0:T(8,128)(2,1)}, u32[]{:S(2)}) copy-start(bf16[128,128]{1,0:T(8,128)(2,1)} %param.18) | copy-start | bytes 98308
  3.1 37.8 %copy-start.1 = (bf16[128,128]{1,0:T(8,128)(2,1)S(1)}, bf16[128,128]{1,0:T(8,128)(2,1)}, u32[]{:S(2)}) copy-start(bf16[128,128]{1,0:T(8,128)(2,1)} %param.19) | copy-start | bytes 98308
  3.1 37.7 %collective-permute-start.3 = (bf16[192,128]{1,0:T(8,128)(2,1)S(1)}, bf16[192,128]{1,0:T(8,128)(2,1)S(1)}, u32[]{:S(2)}, u32[]{:S(2)}) collective-permute-start(bf16[192,128]{1,0:T(8,128)(2,1)S(1)} %get-tuple-element.103), channel_id=1, source_target_pairs={{2,0},{3,1},{4,2},{5,3},{6,4},{7,5},{8,6},{9,7},{10,8},{11,9},{12,... | collective-permute-start | bytes 147464 | tf_op jit(solution)/shard_map/ppermute | solution.py:10
  19.8 21.0 %collective-permute-start.2 = (bf16[192,128]{1,0:T(8,128)(2,1)S(1)}, bf16[192,128]{1,0:T(8,128)(2,1)S(1)}, u32[]{:S(2)}, u32[]{:S(2)}) collective-permute-start(bf16[192,128]{1,0:T(8,128)(2,1)S(1)} %get-tuple-element.104), channel_id=1, source_target_pairs={{0,2},{1,3},{2,4},{3,5},{4,6},{5,7},{6,8},{7,9},{8,10},{9,11},{10,... | collective-permute-start | bytes 147464 | tf_op jit(solution)/shard_map/ppermute | solution.py:10
  21.7 19.1 %collective-permute-start.1 = (bf16[192,128]{1,0:T(8,128)(2,1)S(1)}, bf16[192,128]{1,0:T(8,128)(2,1)S(1)}, u32[]{:S(2)}, u32[]{:S(2)}) collective-permute-start(bf16[192,128]{1,0:T(8,128)(2,1)S(1)} %get-tuple-element.105), channel_id=1, source_target_pairs={{1,0},{2,1},{3,2},{4,3},{5,4},{6,5},{7,6},{8,7},{9,8},{10,9},{11,1... | collective-permute-start | bytes 147464 | tf_op jit(solution)/shard_map/ppermute | solution.py:10
  29.9 10.8 %collective-permute-start = (bf16[192,128]{1,0:T(8,128)(2,1)S(1)}, bf16[192,128]{1,0:T(8,128)(2,1)S(1)}, u32[]{:S(2)}, u32[]{:S(2)}) collective-permute-start(bf16[192,128]{1,0:T(8,128)(2,1)S(1)} %get-tuple-element.106), channel_id=1, source_target_pairs={{0,1},{1,2},{2,3},{3,4},{4,5},{5,6},{6,7},{7,8},{8,9},{9,10},{10,1... | collective-permute-start | bytes 147464 | tf_op jit(solution)/shard_map/ppermute | solution.py:10
  87.4 15.4 %collective-permute-start.4 = (f32[192,128]{1,0:T(8,128)S(1)}, f32[192,128]{1,0:T(8,128)S(1)}, u32[]{:S(2)}, u32[]{:S(2)}) collective-permute-start(f32[192,128]{1,0:T(8,128)S(1)} %get-tuple-element.101), channel_id=1, source_target_pairs={{1,0},{2,1},{3,2},{4,3},{5,4},{6,5},{7,6},{8,7},{9,8},{10,9},{11,1... | collective-permute-start | bytes 294920 | tf_op jit(solution)/shard_map/ppermute | solution.py:10
  89.3 15.6 %collective-permute-start.7 = (f32[192,128]{1,0:T(8,128)S(1)}, f32[192,128]{1,0:T(8,128)S(1)}, u32[]{:S(2)}, u32[]{:S(2)}) collective-permute-start(f32[192,128]{1,0:T(8,128)S(1)} %get-tuple-element.99), channel_id=1, source_target_pairs={{0,2},{1,3},{2,4},{3,5},{4,6},{5,7},{6,8},{7,9},{8,10},{9,11},{10,... | collective-permute-start | bytes 294920 | tf_op jit(solution)/shard_map/ppermute | solution.py:10
  91.2 11.6 %collective-permute-start.5 = (f32[192,128]{1,0:T(8,128)S(1)}, f32[192,128]{1,0:T(8,128)S(1)}, u32[]{:S(2)}, u32[]{:S(2)}) collective-permute-start(f32[192,128]{1,0:T(8,128)S(1)} %get-tuple-element.100), channel_id=1, source_target_pairs={{0,1},{1,2},{2,3},{3,4},{4,5},{5,6},{6,7},{7,8},{8,9},{9,10},{10,1... | collective-permute-start | bytes 294920 | tf_op jit(solution)/shard_map/ppermute | solution.py:10
  93.6 11.3 %collective-permute-start.6 = (f32[192,128]{1,0:T(8,128)S(1)}, f32[192,128]{1,0:T(8,128)S(1)}, u32[]{:S(2)}, u32[]{:S(2)}) collective-permute-start(f32[192,128]{1,0:T(8,128)S(1)} %get-tuple-element.102), channel_id=1, source_target_pairs={{2,0},{3,1},{4,2},{5,3},{6,4},{7,5},{8,6},{9,7},{10,8},{11,9},{12,... | collective-permute-start | bytes 294920 | tf_op jit(solution)/shard_map/ppermute | solution.py:10
where the time goes:
time: 108 us; the launch traced here: 107 us
  matrix products  46.8 us (43%)
  starting transfers between devices  44.1 us (41%)
  waiting for transfers between devices  10.3 us (10%)
  local copies, waits for them, and re-layouts  4.12 us (4%)
    ppermute x8, starting transfers between devices, shifted(): return lax.ppermute(block, axis, route)  44.1 us
    dot_general x5, matrix products, transposed_product(): jnp.einsum('er,ec->rc', table, lower, preferred_element_type=jnp.float32)  15.2 us
    dot_general x4, matrix products, element_block(): element_in = jnp.dot(table, extended, preferred_element_type=jnp.float32)  14.6 us
    dot_general x5, matrix products, transposed_product(): jnp.einsum('er,ec->rc', table, upper, preferred_element_type=jnp.float32)  13.9 us
    ppermute x8, waiting for transfers between devices, shifted(): return lax.ppermute(block, axis, route)  10.3 us
    squeeze x8, local copies, waits for them, and re-layouts, per_device(): lax.scan(element_block, start_partial, (index_blocks, weight_blocks, visc...  2.94 us
  transfers between devices with their start and end apart: 8, of which 3 were waited for; matrix products, arithmetic and copies ran while one was open for 0% of the time, Pallas kernels for 0%

commit v1 on v0

v1 whole, which is shorter than its diff:
```python
import functools

import jax
import jax.numpy as jnp
from jax import lax
from jax.experimental import pallas as pl
from jax.experimental.pallas import tpu as pltpu
from jax.sharding import PartitionSpec as P

LANES = 128
MESH = pl.DeviceIdType.MESH


def shift_list(region_count):
    return [(region // 2 + 1) * (1 if region % 2 == 0 else -1) for region in range(region_count)]


def contract(lhs, rhs, lhs_dim, rhs_dim):
    return lax.dot_general(
        lhs, rhs, (((lhs_dim,), (rhs_dim,)), ((), ())), preferred_element_type=jnp.float32
    )


def operator_kernel(
    n_curve,
    n_seg,
    live_ref,
    count_ref,
    solution_ref,
    visc_ref,
    index_ref,
    weight_ref,
    mirror_ref,
    viscous_ref,
    pressure_ref,
    out_ref,
    column_ids,
    table,
    mirror_table,
    dofs_t,
    gathered,
    element_out,
    outgoing,
    ghosts,
    back_out,
    back_in,
    send_sem,
    recv_sem,
    back_send_sem,
    back_recv_sem,
):
    owned = solution_ref.shape[0]
    width = solution_ref.shape[1]
    regions, ghost_rows = mirror_ref.shape
    slots, elems = index_ref.shape
    columns = table.shape[0]
    ghost_total = columns - owned
    pad_rows = mirror_table.shape[1] // regions
    devices = n_curve * n_seg
    offsets = shift_list(regions)
    me = lax.axis_index("curve") * n_seg + lax.axis_index("seg")

    def place(device):
        return (device // n_seg, lax.rem(device, n_seg))

    def exists(device):
        return jnp.logical_and(device >= 0, device < devices)

    barrier = pltpu.get_barrier_semaphore()
    for offset in offsets:
        @pl.when(exists(me + offset))
        def _():
            pl.semaphore_signal(barrier, inc=1, device_id=place(me + offset), device_id_type=MESH)

    rows = lax.broadcasted_iota(jnp.int32, (owned, ghost_rows), 0)
    entry = lax.broadcasted_iota(jnp.int32, (1, ghost_rows), 1)
    mirror_table[...] = jnp.zeros_like(mirror_table)
    for region in range(regions):
        picks = jnp.where(entry < live_ref[0, region], mirror_ref[region : region + 1, :], -1)
        hit = (rows == picks).astype(jnp.float32).astype(jnp.bfloat16)
        mirror_table[:, region * pad_rows : region * pad_rows + ghost_rows] = hit
    dofs_t[:, :owned] = solution_ref[...].astype(jnp.float32).T.astype(jnp.bfloat16)
    listed = contract(dofs_t[:, :owned], mirror_table[...], 1, 0)
    outgoing[...] = listed.T.astype(jnp.bfloat16)

    peers = sum(exists(me + offset).astype(jnp.int32) for offset in offsets)
    pl.semaphore_wait(barrier, peers)

    def ghost_copy(region):
        return pltpu.make_async_remote_copy(
            src_ref=outgoing.at[pl.ds(region * pad_rows, ghost_rows)],
            dst_ref=ghosts.at[pl.ds(region * ghost_rows, ghost_rows)],
            send_sem=send_sem.at[region],
            recv_sem=recv_sem.at[region],
            device_id=place(me + offsets[region]),
            device_id_type=MESH,
        )

    for region in range(regions):
        @pl.when(exists(me + offsets[region]))
        def _():
            ghost_copy(region).start()

        @pl.when(jnp.logical_not(exists(me - offsets[region])))
        def _():
            ghosts[region * ghost_rows : (region + 1) * ghost_rows] = jnp.zeros(
                (ghost_rows, width), jnp.bfloat16
            )

    sub = 16
    column_ids[...] = lax.broadcasted_iota(jnp.int32, column_ids.shape, 0).astype(jnp.int16)
    count = count_ref[0]
    chunk = min(512, elems)

    def build(step, carry):
        for group in range(chunk // LANES):
            start = pl.multiple_of(step * chunk + group * LANES, LANES)
            lanes = pl.ds(start, LANES)
            live = (lax.broadcasted_iota(jnp.int32, (1, LANES), 1) + start) < count
            index = [index_ref[slot : slot + 1, lanes] for slot in range(slots)]
            raw = [
                jnp.where(live, weight_ref[slot : slot + 1, lanes].astype(jnp.float32) * 0.125, 0.0)
                for slot in range(slots)
            ]
            merged = []
            for slot in range(slots):
                value = raw[slot]
                for other in range(slot):
                    value = value + jnp.where(index[other] == index[slot], raw[other], 0.0)
                merged.append(value)
            ids = [jnp.broadcast_to(i, (sub, LANES)).astype(jnp.int16) for i in index]
            wts = [jnp.broadcast_to(v, (sub, LANES)).astype(jnp.bfloat16) for v in merged]
            for block in range(columns // sub):
                here = slice(block * sub, (block + 1) * sub)
                ident = column_ids[here, :]
                value = jnp.zeros((sub, LANES), jnp.bfloat16)
                first = 0 if block * sub < owned else 1
                for slot in range(first, slots):
                    value = jnp.where(ident == ids[slot], wts[slot], value)
                table[here, lanes] = value
        lanes = pl.ds(pl.multiple_of(step * chunk, chunk), chunk)
        gathered[:, lanes] = contract(dofs_t[:, :owned], table[:owned, lanes], 1, 0)
        return carry

    lax.fori_loop(0, elems // chunk, build, 0)

    for region in range(regions):
        @pl.when(exists(me - offsets[region]))
        def _():
            ghost_copy(region).wait_recv()

    dofs_t[:, owned:] = ghosts[...].astype(jnp.float32).T.astype(jnp.bfloat16)
    viscous = viscous_ref[...].astype(jnp.float32).T.astype(jnp.bfloat16)
    pressure = pressure_ref[...].astype(jnp.float32).T.astype(jnp.bfloat16)

    def apply(step, carry):
        lanes = pl.ds(pl.multiple_of(step * chunk, chunk), chunk)
        total = gathered[:, lanes] + contract(dofs_t[:, owned:], table[owned:, lanes], 1, 0)
        element_in = total.astype(jnp.bfloat16)
        result = contract(viscous, element_in, 1, 0) * visc_ref[:, lanes]
        result = result + contract(pressure, element_in, 1, 0)
        element_out[:, lanes] = result.astype(jnp.bfloat16)
        return carry

    lax.fori_loop(0, elems // chunk, apply, 0)

    def back_copy(region):
        return pltpu.make_async_remote_copy(
            src_ref=back_out.at[pl.ds(region * ghost_rows, ghost_rows)],
            dst_ref=back_in.at[pl.ds(region * pad_rows, ghost_rows)],
            send_sem=back_send_sem.at[region],
            recv_sem=back_recv_sem.at[region],
            device_id=place(me - offsets[region]),
            device_id_type=MESH,
        )

    for region in range(regions):
        back_in[region * pad_rows + ghost_rows : (region + 1) * pad_rows] = jnp.zeros(
            (pad_rows - ghost_rows, width), jnp.bfloat16
        )

        @pl.when(jnp.logical_not(exists(me + offsets[region])))
        def _():
            back_in[region * pad_rows : region * pad_rows + ghost_rows] = jnp.zeros(
                (ghost_rows, width), jnp.bfloat16
            )

    ghost_part = contract(element_out[...], table[owned:], 1, 1)
    back_out[...] = ghost_part.T.astype(jnp.bfloat16)
    for region in range(regions):
        @pl.when(exists(me - offsets[region]))
        def _():
            back_copy(region).start()

    own_part = contract(element_out[...], table[:owned], 1, 1)
    out_ref[...] = own_part.T

    for region in range(regions):
        @pl.when(exists(me + offsets[region]))
        def _():
            back_copy(region).wait_recv()

    out_ref[...] += contract(mirror_table[...], back_in[...], 1, 0)

    for region in range(regions):
        @pl.when(exists(me + offsets[region]))
        def _():
            ghost_copy(region).wait_send()

        @pl.when(exists(me - offsets[region]))
        def _():
            back_copy(region).wait_send()


def per_device(
    n_curve,
    n_seg,
    solution,
    viscosity,
    slot_index,
    slot_weight,
    mirror_rows,
    ghost_live,
    cell_count,
    viscous_block,
    pressure_block,
):
    owned, width = solution.shape
    elems, slots = slot_index.shape
    regions, ghost_rows = mirror_rows.shape[1:]
    pad_rows = -(-ghost_rows // LANES) * LANES
    columns = owned + regions * ghost_rows
    vmem = pl.BlockSpec(memory_space=pltpu.VMEM)
    smem = pl.BlockSpec(memory_space=pltpu.SMEM)
    bf16 = jnp.bfloat16
    return pl.pallas_call(
        functools.partial(operator_kernel, n_curve, n_seg),
        out_shape=jax.ShapeDtypeStruct((owned, width), jnp.float32),
        in_specs=[smem, smem] + [vmem] * 7,
        out_specs=vmem,
        scratch_shapes=[
            pltpu.VMEM((columns, LANES), jnp.int16),
            pltpu.VMEM((columns, elems), bf16),
            pltpu.VMEM((owned, regions * pad_rows), bf16),
            pltpu.VMEM((width, columns), bf16),
            pltpu.VMEM((width, elems), jnp.float32),
            pltpu.VMEM((width, elems), bf16),
            pltpu.VMEM((regions * pad_rows, width), bf16),
            pltpu.VMEM((regions * ghost_rows, width), bf16),
            pltpu.VMEM((regions * ghost_rows, width), bf16),
            pltpu.VMEM((regions * pad_rows, width), bf16),
            pltpu.SemaphoreType.DMA((regions,)),
            pltpu.SemaphoreType.DMA((regions,)),
            pltpu.SemaphoreType.DMA((regions,)),
            pltpu.SemaphoreType.DMA((regions,)),
        ],
        compiler_params=pltpu.CompilerParams(
            collective_id=0, has_side_effects=True, vmem_limit_bytes=48 * 1024 * 1024
        ),
    )(
        ghost_live,
        cell_count,
        solution,
        viscosity.reshape(1, elems),
        slot_index.T,
        slot_weight.T,
        mirror_rows.reshape(regions, ghost_rows),
        viscous_block,
        pressure_block,
    )


def solution(mesh):
    return jax.shard_map(
        functools.partial(per_device, mesh.shape["curve"], mesh.shape["seg"]),
        mesh=mesh,
        in_specs=(
            P(("curve", "seg"), None),
            P(("curve", "seg")),
            P(("curve", "seg"), None),
            P(("curve", "seg"), None),
            P(("curve", "seg"), None, None),
            P(("curve", "seg"), None),
            P(("curve", "seg")),
            P(),
            P(),
        ),
        out_specs=P(("curve", "seg"), None),
        check_vma=False,
    )
```

time: 108 us -> 42.8 us (0.40)
  the two profiles are of different devices: /device:TPU:32 before, /device:TPU:56 now
where the time goes in v1:
time: 42.8 us; the launch traced here: 42 us
  Pallas kernels  35.2 us (82%)
  local copies, waits for them, and re-layouts  6.19 us (14%)
  between operations  0.68 us (2%)
    pallas_call x1, Pallas kernels, per_device(): pl.pallas_call(functools.partial(operator_kernel, n_curve, n_seg), out_sh...  35.2 us
    unnamed x17, local copies, waits for them, and re-layouts  6.19 us

profile of v1, /device:TPU:56, one launch (start us, length us, event | category | flops | bytes accessed | tf_op | source)
XLA Modules:
  0.0 42.0 jit_solution(7512196987181259135)
XLA Ops:
  0.7 0.0 copy-start.6
  0.7 0.0 copy-start.7
  0.7 0.7 %copy-done.6 = s32[1,4,192]{2,1,0:T(4,128)S(1)} copy-done((s32[1,4,192]{2,1,0:T(4,128)S(1)}, s32[1,4,192]{2,1,0:T(4,128)}, u32[]{:S(2)}) %copy-start.6) | copy-done | bytes 3096
  1.3 0.0 copy-done.7
  1.3 0.0 copy-start
  1.3 0.9 %copy-done = bf16[512,128]{1,0:T(8,128)(2,1)S(1)} copy-done((bf16[512,128]{1,0:T(8,128)(2,1)S(1)}, bf16[512,128]{1,0:T(8,128)(2,1)}, u32[]{:S(2)}) %copy-start) | copy-done | bytes 131096
  2.2 0.0 copy-start.1
  2.2 0.8 %copy-done.1 = s32[4096,4]{0,1:T(4,128)S(1)} copy-done((s32[4096,4]{0,1:T(4,128)S(1)}, s32[4096,4]{0,1:T(4,128)}, u32[]{:S(2)}) %copy-start.1) | copy-done | bytes 65560
  3.1 0.0 copy-start.2
  3.1 0.8 %copy-done.2 = s32[4096,4]{0,1:T(4,128)S(1)} copy-done((s32[4096,4]{0,1:T(4,128)S(1)}, s32[4096,4]{0,1:T(4,128)}, u32[]{:S(2)}) %copy-start.2) | copy-done | bytes 65560
  3.9 0.0 copy-start.3
  3.9 0.8 %copy-done.3 = bf16[128,128]{1,0:T(8,128)(2,1)S(1)} copy-done((bf16[128,128]{1,0:T(8,128)(2,1)S(1)}, bf16[128,128]{1,0:T(8,128)(2,1)}, u32[]{:S(2)}) %copy-start.3) | copy-done | bytes 32792
  4.7 0.0 copy-start.4
  4.7 0.8 %copy-done.4 = bf16[128,128]{1,0:T(8,128)(2,1)S(1)} copy-done((bf16[128,128]{1,0:T(8,128)(2,1)S(1)}, bf16[128,128]{1,0:T(8,128)(2,1)}, u32[]{:S(2)}) %copy-start.4) | copy-done | bytes 32792
  5.4 0.0 copy-start.5
  5.4 0.7 %copy-done.5 = f32[4096]{0:T(1024)S(1)} copy-done((f32[4096]{0:T(1024)S(1)}, f32[4096]{0:T(1024)}, u32[]{:S(2)}) %copy-start.5) | copy-done | bytes 16408
  6.2 35.2 %shard_map.91 = f32[512,128]{1,0:T(8,128)S(1)} custom-call(s32[1,4]{1,0:T(1,128)S(1)} %copy-done.7, s32[1]{0:T(128)S(6)} %copy.11.count_ref, bf16[512,128]{1,0:T(8,128)(2,1)S(1)} %copy-done, f32[1,4096]{1,0:T(1,128)S(1)} %bitcast.6, s32[4,4096]{1,0:T(4,128)S(1)} %bitcast.4, s32[4,4096]{1,0:T(4,128)S(1)} %bitcast.5, s32[4,192]{1,0:T(4,128)S(1)} %bitcast.7, ...), custom_call_target="tpu_custom_call" | custom-call | tf_op jit(solution)/shard_map/pallas_call | solution.py:236
  41.3 0.7 %copy.12 = f32[512,128]{1,0:T(8,128)} copy(f32[512,128]{1,0:T(8,128)S(1)} %shard_map.91) | data formatting | bytes 524288
Async XLA Ops:
  0.7 0.7 %copy-start.6 = (s32[1,4,192]{2,1,0:T(4,128)S(1)}, s32[1,4,192]{2,1,0:T(4,128)}, u32[]{:S(2)}) copy-start(s32[1,4,192]{2,1,0:T(4,128)} %param.13) | copy-start | bytes 9220
  0.7 0.7 %copy-start.7 = (s32[1,4]{1,0:T(1,128)S(1)}, s32[1,4]{1,0:T(1,128)}, u32[]{:S(2)}) copy-start(s32[1,4]{1,0:T(1,128)} %live_ref.1) | copy-start | bytes 52
  1.3 0.9 %copy-start = (bf16[512,128]{1,0:T(8,128)(2,1)S(1)}, bf16[512,128]{1,0:T(8,128)(2,1)}, u32[]{:S(2)}) copy-start(bf16[512,128]{1,0:T(8,128)(2,1)} %solution_ref.1) | copy-start | bytes 393220
  2.2 0.8 %copy-start.1 = (s32[4096,4]{0,1:T(4,128)S(1)}, s32[4096,4]{0,1:T(4,128)}, u32[]{:S(2)}) copy-start(s32[4096,4]{0,1:T(4,128)} %param.11) | copy-start | bytes 196612
  3.1 0.8 %copy-start.2 = (s32[4096,4]{0,1:T(4,128)S(1)}, s32[4096,4]{0,1:T(4,128)}, u32[]{:S(2)}) copy-start(s32[4096,4]{0,1:T(4,128)} %param.12) | copy-start | bytes 196612
  3.9 0.8 %copy-start.3 = (bf16[128,128]{1,0:T(8,128)(2,1)S(1)}, bf16[128,128]{1,0:T(8,128)(2,1)}, u32[]{:S(2)}) copy-start(bf16[128,128]{1,0:T(8,128)(2,1)} %viscous_ref.1) | copy-start | bytes 98308
  4.7 0.8 %copy-start.4 = (bf16[128,128]{1,0:T(8,128)(2,1)S(1)}, bf16[128,128]{1,0:T(8,128)(2,1)}, u32[]{:S(2)}) copy-start(bf16[128,128]{1,0:T(8,128)(2,1)} %pressure_ref.1) | copy-start | bytes 98308
  5.4 0.7 %copy-start.5 = (f32[4096]{0:T(1024)S(1)}, f32[4096]{0:T(1024)}, u32[]{:S(2)}) copy-start(f32[4096]{0:T(1024)} %param.10) | copy-start | bytes 49156

commit v2 on v1

v2 whole, which is shorter than its diff:
```python
import functools

import jax
import jax.numpy as jnp
from jax import lax
from jax.experimental import pallas as pl
from jax.experimental.pallas import tpu as pltpu
from jax.sharding import PartitionSpec as P

LANES = 128
MESH = pl.DeviceIdType.MESH


def shift_list(region_count):
    return [(region // 2 + 1) * (1 if region % 2 == 0 else -1) for region in range(region_count)]


def contract(lhs, rhs, lhs_dim, rhs_dim):
    return lax.dot_general(
        lhs, rhs, (((lhs_dim,), (rhs_dim,)), ((), ())), preferred_element_type=jnp.float32
    )


def operator_kernel(
    n_curve,
    n_seg,
    count_ref,
    solution_hbm,
    visc_hbm,
    index_hbm,
    weight_hbm,
    mirror_hbm,
    live_hbm,
    viscous_hbm,
    pressure_hbm,
    out_ref,
    solution_ref,
    visc_ref,
    index_ref,
    weight_ref,
    mirror_ref,
    live_ref,
    viscous_ref,
    pressure_ref,
    table,
    mirror_table,
    dofs_t,
    gathered,
    element_out,
    outgoing,
    ghosts,
    back_out,
    back_in,
    load_sem,
    send_sem,
    recv_sem,
    back_send_sem,
    back_recv_sem,
):
    owned, width = solution_ref.shape
    regions, ghost_rows = mirror_ref.shape
    slots, elems = index_ref.shape
    groups, columns, lanes_of = table.shape
    pad_rows = mirror_table.shape[1] // regions
    devices = n_curve * n_seg
    offsets = shift_list(regions)
    order = [k for k in range(regions) if offsets[k] > 0]
    half = len(order)
    order = order + [k for k in range(regions) if offsets[k] < 0]
    place_of = {region: pos for pos, region in enumerate(order)}
    split = half * ghost_rows
    me = lax.axis_index("curve") * n_seg + lax.axis_index("seg")

    def place(device):
        return (device // n_seg, lax.rem(device, n_seg))

    def exists(device):
        return jnp.logical_and(device >= 0, device < devices)

    barrier = pltpu.get_barrier_semaphore()
    for offset in offsets:
        @pl.when(exists(me + offset))
        def _():
            pl.semaphore_signal(barrier, inc=1, device_id=place(me + offset), device_id_type=MESH)

    pairs = [
        (mirror_hbm, mirror_ref),
        (live_hbm, live_ref),
        (solution_hbm, solution_ref),
        (index_hbm, index_ref),
        (weight_hbm, weight_ref),
        (visc_hbm, visc_ref),
        (viscous_hbm, viscous_ref),
        (pressure_hbm, pressure_ref),
    ]
    loads = [
        pltpu.make_async_copy(source, target, load_sem.at[pos])
        for pos, (source, target) in enumerate(pairs)
    ]
    for load in loads:
        load.start()

    sub = 16
    row16 = lax.broadcasted_iota(jnp.int32, (sub, lanes_of), 0).astype(jnp.int16)
    one = jnp.ones((sub, lanes_of), jnp.bfloat16)
    zero = jnp.zeros((sub, lanes_of), jnp.bfloat16)

    for load in loads[:3]:
        load.wait()
    for pos, region in enumerate(order):
        for part in range(pad_rows // LANES):
            first = part * LANES
            size = min(LANES, ghost_rows - first)
            entry = lax.broadcasted_iota(jnp.int32, (1, LANES), 1) + first
            picks = mirror_ref[region : region + 1, first : first + size]
            if size < LANES:
                picks = jnp.concatenate([picks, jnp.full((1, LANES - size), -1, jnp.int32)], axis=1)
            limit = jnp.minimum(live_ref[0:1, region : region + 1], ghost_rows)
            picks = jnp.where(entry < limit, picks, -1)
            picks = jnp.broadcast_to(picks, (sub, LANES)).astype(jnp.int16) - row16
            for block in range(owned // sub):
                hit = jnp.where(picks == jnp.int16(block * sub), one, zero)
                start = pos * pad_rows + first
                mirror_table[block * sub : (block + 1) * sub, start : start + LANES] = hit
    dofs_t[:, :owned] = solution_ref[...].astype(jnp.float32).T.astype(jnp.bfloat16)
    listed = contract(dofs_t[:, :owned], mirror_table[...], 1, 0)
    outgoing[...] = listed.T.astype(jnp.bfloat16)

    peers = sum(exists(me + offset).astype(jnp.int32) for offset in offsets)
    pl.semaphore_wait(barrier, peers)

    def ghost_copy(region):
        pos = place_of[region]
        return pltpu.make_async_remote_copy(
            src_ref=outgoing.at[pl.ds(pos * pad_rows, ghost_rows)],
            dst_ref=ghosts.at[pl.ds(pos * ghost_rows, ghost_rows)],
            send_sem=send_sem.at[region],
            recv_sem=recv_sem.at[region],
            device_id=place(me + offsets[region]),
            device_id_type=MESH,
        )

    for region in order:
        @pl.when(exists(me + offsets[region]))
        def _():
            ghost_copy(region).start()

    for pos, region in enumerate(order):
        @pl.when(jnp.logical_not(exists(me - offsets[region])))
        def _():
            ghosts[pos * ghost_rows : (pos + 1) * ghost_rows] = jnp.zeros(
                (ghost_rows, width), jnp.bfloat16
            )

        back_in[pos * pad_rows + ghost_rows : (pos + 1) * pad_rows] = jnp.zeros(
            (pad_rows - ghost_rows, width), jnp.bfloat16
        )

        @pl.when(jnp.logical_not(exists(me + offsets[region])))
        def _():
            back_in[pos * pad_rows : pos * pad_rows + ghost_rows] = jnp.zeros(
                (ghost_rows, width), jnp.bfloat16
            )

    for load in loads[3:5]:
        load.wait()
    per_step = min(4, groups)
    chunk = per_step * lanes_of
    count = count_ref[0]

    def moved(index):
        result = index
        for k in range(regions):
            shift = (place_of[k] - k) * ghost_rows
            if shift:
                low = owned + k * ghost_rows
                inside = jnp.logical_and(index >= low, index < low + ghost_rows)
                result = jnp.where(inside, index + shift, result)
        return result

    def build(step, carry):
        for inner in range(per_step):
            group = step * per_step + inner
            start = pl.multiple_of(group * lanes_of, lanes_of)
            lanes = pl.ds(start, lanes_of)
            live = (lax.broadcasted_iota(jnp.int32, (1, lanes_of), 1) + start) < count
            index = [moved(index_ref[slot : slot + 1, lanes]) for slot in range(slots)]
            raw = [
                jnp.where(live, weight_ref[slot : slot + 1, lanes].astype(jnp.float32) * 0.125, 0.0)
                for slot in range(slots)
            ]
            merged = []
            for slot in range(slots):
                value = raw[slot]
                for other in range(slot):
                    value = value + jnp.where(index[other] == index[slot], raw[other], 0.0)
                merged.append(value)
            shape = (sub, lanes_of)
            ids = [jnp.broadcast_to(i, shape).astype(jnp.int16) - row16 for i in index]
            wts = [jnp.broadcast_to(v, shape).astype(jnp.bfloat16) for v in merged]
            for block in range(columns // sub):
                value = zero
                for slot in range(0 if block * sub < owned else 1, slots):
                    value = jnp.where(ids[slot] == jnp.int16(block * sub), wts[slot], value)
                table[group, block * sub : (block + 1) * sub, :] = value
        gathered[:, step_lanes(step)] = contract(
            dofs_t[:, :owned], rows_of(step, 0, owned), 1, 0
        )
        return carry

    def step_lanes(step):
        return pl.ds(pl.multiple_of(step * chunk, chunk), chunk)

    def rows_of(step, low, high):
        return jnp.concatenate(
            [table[step * per_step + inner, low:high, :] for inner in range(per_step)], axis=1
        )

    steps = groups // per_step
    lax.fori_loop(0, steps, build, 0)

    def receive(chosen):
        for region in chosen:
            @pl.when(exists(me - offsets[region]))
            def _():
                ghost_copy(region).wait_recv()

    receive(order[:half])
    middle = owned + split
    dofs_t[:, owned:middle] = ghosts[:split].astype(jnp.float32).T.astype(jnp.bfloat16)

    def lower_part(step, carry):
        gathered[:, step_lanes(step)] += contract(
            dofs_t[:, owned:middle], rows_of(step, owned, middle), 1, 0
        )
        return carry

    lax.fori_loop(0, steps, lower_part, 0)
    for load in loads[5:]:
        load.wait()
    viscous = viscous_ref[...].astype(jnp.float32).T.astype(jnp.bfloat16)
    pressure = pressure_ref[...].astype(jnp.float32).T.astype(jnp.bfloat16)

    receive(order[half:])
    dofs_t[:, middle:] = ghosts[split:].astype(jnp.float32).T.astype(jnp.bfloat16)

    def apply(step, carry):
        lanes = step_lanes(step)
        total = gathered[:, lanes] + contract(
            dofs_t[:, middle:], rows_of(step, middle, columns), 1, 0
        )
        element_in = total.astype(jnp.bfloat16)
        result = contract(viscous, element_in, 1, 0) * visc_ref[:, lanes]
        result = result + contract(pressure, element_in, 1, 0)
        element_out[:, lanes] = result.astype(jnp.bfloat16)
        return carry

    lax.fori_loop(0, steps, apply, 0)

    def back_copy(region):
        pos = place_of[region]
        return pltpu.make_async_remote_copy(
            src_ref=back_out.at[pl.ds(pos * ghost_rows, ghost_rows)],
            dst_ref=back_in.at[pl.ds(pos * pad_rows, ghost_rows)],
            send_sem=back_send_sem.at[region],
            recv_sem=back_recv_sem.at[region],
            device_id=place(me - offsets[region]),
            device_id_type=MESH,
        )

    def scatter(low, high):
        rows = jnp.concatenate([table[group, low:high, :] for group in range(groups)], axis=1)
        return contract(element_out[...], rows, 1, 1).T

    back_out[split:] = scatter(middle, columns).astype(jnp.bfloat16)
    for region in order[half:]:
        @pl.when(exists(me - offsets[region]))
        def _():
            back_copy(region).start()

    back_out[:split] = scatter(owned, middle).astype(jnp.bfloat16)
    for region in order[:half]:
        @pl.when(exists(me - offsets[region]))
        def _():
            back_copy(region).start()

    out_ref[...] = scatter(0, owned)

    for chosen, low in ((order[:half], 0), (order[half:], half * pad_rows)):
        for region in chosen:
            @pl.when(exists(me + offsets[region]))
            def _():
                back_copy(region).wait_recv()

        high = low + half * pad_rows
        out_ref[...] += contract(mirror_table[:, low:high], back_in[low:high], 1, 0)

    for region in range(regions):
        @pl.when(exists(me + offsets[region]))
        def _():
            ghost_copy(region).wait_send()

        @pl.when(exists(me - offsets[region]))
        def _():
            back_copy(region).wait_send()


def per_device(
    n_curve,
    n_seg,
    solution,
    viscosity,
    slot_index,
    slot_weight,
    mirror_rows,
    ghost_live,
    cell_count,
    viscous_block,
    pressure_block,
):
    owned, width = solution.shape
    elems, slots = slot_index.shape
    regions, ghost_rows = mirror_rows.shape[1:]
    pad_rows = -(-ghost_rows // LANES) * LANES
    columns = owned + regions * ghost_rows
    bf16 = jnp.bfloat16
    i32 = jnp.int32
    f32 = jnp.float32
    return pl.pallas_call(
        functools.partial(operator_kernel, n_curve, n_seg),
        out_shape=jax.ShapeDtypeStruct((owned, width), jnp.float32),
        in_specs=[pl.BlockSpec(memory_space=pltpu.SMEM)]
        + [pl.BlockSpec(memory_space=pltpu.HBM)] * 8,
        out_specs=pl.BlockSpec(memory_space=pltpu.VMEM),
        scratch_shapes=[
            pltpu.VMEM((owned, width), bf16),
            pltpu.VMEM((1, elems), f32),
            pltpu.VMEM((slots, elems), i32),
            pltpu.VMEM((slots, elems), i32),
            pltpu.VMEM((regions, ghost_rows), i32),
            pltpu.VMEM((1, regions), i32),
            pltpu.VMEM((width, width), bf16),
            pltpu.VMEM((width, width), bf16),
            pltpu.VMEM((elems // LANES, columns, LANES), bf16),
            pltpu.VMEM((owned, regions * pad_rows), bf16),
            pltpu.VMEM((width, columns), bf16),
            pltpu.VMEM((width, elems), f32),
            pltpu.VMEM((width, elems), bf16),
            pltpu.VMEM((regions * pad_rows, width), bf16),
            pltpu.VMEM((regions * ghost_rows, width), bf16),
            pltpu.VMEM((regions * ghost_rows, width), bf16),
            pltpu.VMEM((regions * pad_rows, width), bf16),
            pltpu.SemaphoreType.DMA((8,)),
            pltpu.SemaphoreType.DMA((regions,)),
            pltpu.SemaphoreType.DMA((regions,)),
            pltpu.SemaphoreType.DMA((regions,)),
            pltpu.SemaphoreType.DMA((regions,)),
        ],
        compiler_params=pltpu.CompilerParams(
            collective_id=0, has_side_effects=True, vmem_limit_bytes=48 * 1024 * 1024
        ),
    )(
        cell_count,
        *(
            pltpu.with_memory_space_constraint(operand, pltpu.HBM)
            for operand in (
                solution,
                viscosity.reshape(1, elems),
                slot_index.T,
                slot_weight.T,
                mirror_rows.reshape(regions, ghost_rows),
                ghost_live,
                viscous_block,
                pressure_block,
            )
        )
    )


def solution(mesh):
    return jax.shard_map(
        functools.partial(per_device, mesh.shape["curve"], mesh.shape["seg"]),
        mesh=mesh,
        in_specs=(
            P(("curve", "seg"), None),
            P(("curve", "seg")),
            P(("curve", "seg"), None),
            P(("curve", "seg"), None),
            P(("curve", "seg"), None, None),
            P(("curve", "seg"), None),
            P(("curve", "seg")),
            P(),
            P(),
        ),
        out_specs=P(("curve", "seg"), None),
        check_vma=False,
    )
```

time: 42.8 us -> 35.3 us (0.82); the launches traced: 42 us -> 35.2 us
  local copies, waits for them, and re-layouts: 6.19 us -> 0.71 us
  Pallas kernels: 35.2 us -> 33.8 us
    unnamed x17 -> x1, local copies, waits for them, and re-layouts: 6.19 us -> 0.71 us
    pallas_call x1, Pallas kernels: 35.2 us -> 33.8 us  [per_device(): pl.pallas_call(functools.partial(operator_kernel, n_curve, n_seg), out_sh...]
where the time goes in v2:
time: 35.3 us; the launch traced here: 35.2 us
  Pallas kernels  33.8 us (96%)
  local copies, waits for them, and re-layouts  0.71 us (2%)
  between operations  0.66 us (2%)
    pallas_call x1, Pallas kernels, per_device(): pl.pallas_call(functools.partial(operator_kernel, n_curve, n_seg), out_sh...  33.8 us

profile of v2, /device:TPU:56, one launch (start us, length us, event | category | flops | bytes accessed | tf_op | source)
XLA Modules:
  0.0 35.2 jit_solution(12392360874451778798)
XLA Ops:
  0.7 33.8 %shard_map.91 = f32[512,128]{1,0:T(8,128)S(1)} custom-call(s32[1]{0:T(128)S(6)} %copy.11.count_ref, bf16[512,128]{1,0:T(8,128)(2,1)} %solution_hbm.1, f32[1,4096]{1,0:T(1,128)} %bitcast.6, s32[4,4096]{1,0:T(4,128)} %bitcast.4, s32[4,4096]{1,0:T(4,128)} %bitcast.5, s32[4,192]{1,0:T(4,128)} %bitcast.7, s32[1,4]{1,0:T(1,128)} %live_hbm.1, ...), custom_call_target="tpu_custom_call" | custom-call | tf_op jit(solution)/shard_map/pallas_call | solution.py:329
  34.5 0.7 %copy.12 = f32[512,128]{1,0:T(8,128)} copy(f32[512,128]{1,0:T(8,128)S(1)} %shard_map.91) | data formatting | bytes 524288

commit v3 on v2

--- a/solution.py
+++ b/solution.py
@@ -178,10 +178,25 @@
                 result = jnp.where(inside, index + shift, result)
         return result
 
-    def build(step, carry):
+    def step_lanes(step):
+        return pl.ds(step * chunk, chunk) if isinstance(step, int) else pl.ds(
+            pl.multiple_of(step * chunk, chunk), chunk
+        )
+
+    def rows_of(step, low, high):
+        return jnp.concatenate(
+            [table[step * per_step + inner, low:high, :] for inner in range(per_step)], axis=1
+        )
+
+    def owned_product(step):
+        return contract(dofs_t[:, :owned], rows_of(step, 0, owned), 1, 0)
+
+    def build(step):
         for inner in range(per_step):
             group = step * per_step + inner
-            start = pl.multiple_of(group * lanes_of, lanes_of)
+            start = group * lanes_of
+            if not isinstance(step, int):
+                start = pl.multiple_of(start, lanes_of)
             lanes = pl.ds(start, lanes_of)
             live = (lax.broadcasted_iota(jnp.int32, (1, lanes_of), 1) + start) < count
             index = [moved(index_ref[slot : slot + 1, lanes]) for slot in range(slots)]
@@ -203,21 +218,17 @@
                 for slot in range(0 if block * sub < owned else 1, slots):
                     value = jnp.where(ids[slot] == jnp.int16(block * sub), wts[slot], value)
                 table[group, block * sub : (block + 1) * sub, :] = value
-        gathered[:, step_lanes(step)] = contract(
-            dofs_t[:, :owned], rows_of(step, 0, owned), 1, 0
-        )
+
+    def build_behind(step, carry):
+        product = owned_product(step - 1)
+        build(step)
+        gathered[:, step_lanes(step - 1)] = product
         return carry
 
-    def step_lanes(step):
-        return pl.ds(pl.multiple_of(step * chunk, chunk), chunk)
-
-    def rows_of(step, low, high):
-        return jnp.concatenate(
-            [table[step * per_step + inner, low:high, :] for inner in range(per_step)], axis=1
-        )
-
     steps = groups // per_step
-    lax.fori_loop(0, steps, build, 0)
+    build(0)
+    lax.fori_loop(1, steps, build_behind, 0)
+    gathered[:, step_lanes(steps - 1)] = owned_product(steps - 1)
 
     def receive(chosen):
         for region in chosen:
@@ -229,13 +240,10 @@
     middle = owned + split
     dofs_t[:, owned:middle] = ghosts[:split].astype(jnp.float32).T.astype(jnp.bfloat16)
 
-    def lower_part(step, carry):
+    for step in range(steps):
         gathered[:, step_lanes(step)] += contract(
             dofs_t[:, owned:middle], rows_of(step, owned, middle), 1, 0
         )
-        return carry
-
-    lax.fori_loop(0, steps, lower_part, 0)
     for load in loads[5:]:
         load.wait()
     viscous = viscous_ref[...].astype(jnp.float32).T.astype(jnp.bfloat16)
@@ -244,7 +252,7 @@
     receive(order[half:])
     dofs_t[:, middle:] = ghosts[split:].astype(jnp.float32).T.astype(jnp.bfloat16)
 
-    def apply(step, carry):
+    for step in range(steps):
         lanes = step_lanes(step)
         total = gathered[:, lanes] + contract(
             dofs_t[:, middle:], rows_of(step, middle, columns), 1, 0
@@ -253,9 +261,6 @@
         result = contract(viscous, element_in, 1, 0) * visc_ref[:, lanes]
         result = result + contract(pressure, element_in, 1, 0)
         element_out[:, lanes] = result.astype(jnp.bfloat16)
-        return carry
-
-    lax.fori_loop(0, steps, apply, 0)
 
     def back_copy(region):
         pos = place_of[region]

time: 35.3 us -> 33.4 us (0.946)
  Pallas kernels: 33.8 us -> 31.6 us
    pallas_call x1, Pallas kernels: 33.8 us -> 31.6 us  [per_device(): pl.pallas_call(functools.partial(operator_kernel, n_curve, n_seg), out_sh...]
where the time goes in v3:
time: 33.4 us; the launch traced here: 32.9 us
  Pallas kernels  31.6 us (95%)
  local copies, waits for them, and re-layouts  0.71 us (2%)
  between operations  0.66 us (2%)
    pallas_call x1, Pallas kernels, per_device(): pl.pallas_call(functools.partial(operator_kernel, n_curve, n_seg), out_sh...  31.6 us
    unnamed x1, local copies, waits for them, and re-layouts  0.71 us

profile of v3, /device:TPU:56, one launch (start us, length us, event | category | flops | bytes accessed | tf_op | source)
XLA Modules:
  0.0 32.9 jit_solution(14416241761954546323)
XLA Ops:
  0.7 31.6 %shard_map.91 = f32[512,128]{1,0:T(8,128)S(1)} custom-call(s32[1]{0:T(128)S(6)} %copy.11.count_ref, bf16[512,128]{1,0:T(8,128)(2,1)} %solution_hbm.1, f32[1,4096]{1,0:T(1,128)} %bitcast.6, s32[4,4096]{1,0:T(4,128)} %bitcast.4, s32[4,4096]{1,0:T(4,128)} %bitcast.5, s32[4,192]{1,0:T(4,128)} %bitcast.7, s32[1,4]{1,0:T(1,128)} %live_hbm.1, ...), custom_call_target="tpu_custom_call" | custom-call | tf_op jit(solution)/shard_map/pallas_call | solution.py:334
  32.2 0.7 %copy.12 = f32[512,128]{1,0:T(8,128)} copy(f32[512,128]{1,0:T(8,128)S(1)} %shard_map.91) | data formatting | bytes 524288

commit v4 on v3

--- a/solution.py
+++ b/solution.py
@@ -8,6 +8,7 @@
 from jax.sharding import PartitionSpec as P
 
 LANES = 128
+ROW = 12
 MESH = pl.DeviceIdType.MESH
 
 
@@ -49,8 +50,14 @@
     element_out,
     outgoing,
     ghosts,
+    relay,
     back_out,
     back_in,
+    ready_sem,
+    late_sem,
+    relay_send_sem,
+    relay_recv_sem,
+    forward_sem,
     load_sem,
     send_sem,
     recv_sem,
@@ -77,11 +84,44 @@
     def exists(device):
         return jnp.logical_and(device >= 0, device < devices)
 
+    upper = order[half:]
+    reach = max(offsets)
+    hop = (ROW - 1) * n_seg
+
+    def last_in_row(device):
+        return jnp.logical_and(
+            lax.rem(device // n_seg, ROW) == ROW - 1, exists(device)
+        )
+
+    def crosses(device, offset):
+        inside = jnp.logical_and(last_in_row(device), exists(device + offset))
+        return jnp.logical_and(inside, (device + offset) // n_seg != device // n_seg)
+
+    def any_cross(device):
+        return crosses(device, reach)
+
     barrier = pltpu.get_barrier_semaphore()
+
+    def greet(device):
+        pl.semaphore_signal(barrier, inc=1, device_id=place(device), device_id_type=MESH)
+
     for offset in offsets:
-        @pl.when(exists(me + offset))
-        def _():
-            pl.semaphore_signal(barrier, inc=1, device_id=place(me + offset), device_id_type=MESH)
+        wanted = exists(me + offset)
+        if offset > 0:
+            wanted = jnp.logical_and(wanted, jnp.logical_not(crosses(me, offset)))
+
+        @pl.when(wanted)
+        def _():
+            greet(me + offset)
+
+    @pl.when(any_cross(me + hop))
+    def _():
+        greet(me + hop)
+
+    for region in upper:
+        @pl.when(crosses(me + hop, -offsets[region]))
+        def _():
+            greet(me + hop - offsets[region])
 
     pairs = [
         (mirror_hbm, mirror_ref),
@@ -126,8 +166,20 @@
     listed = contract(dofs_t[:, :owned], mirror_table[...], 1, 0)
     outgoing[...] = listed.T.astype(jnp.bfloat16)
 
-    peers = sum(exists(me + offset).astype(jnp.int32) for offset in offsets)
+    peers = any_cross(me).astype(jnp.int32)
+    for offset in offsets:
+        peers = peers + exists(me + offset).astype(jnp.int32)
     pl.semaphore_wait(barrier, peers)
+
+    @pl.when(any_cross(me))
+    def _():
+        pl.semaphore_signal(ready_sem, inc=1, device_id=place(me - hop), device_id_type=MESH)
+
+    for region in upper:
+        @pl.when(crosses(me, -offsets[region]))
+        def _():
+            target = place(me - offsets[region])
+            pl.semaphore_signal(late_sem, inc=1, device_id=target, device_id_type=MESH)
 
     def ghost_copy(region):
         pos = place_of[region]
@@ -140,10 +192,45 @@
             device_id_type=MESH,
         )
 
+    def relay_copy(region):
+        pos = place_of[region]
+        return pltpu.make_async_remote_copy(
+            src_ref=outgoing.at[pl.ds(pos * pad_rows, ghost_rows)],
+            dst_ref=relay.at[pl.ds((pos - half) * ghost_rows, ghost_rows)],
+            send_sem=relay_send_sem.at[region],
+            recv_sem=relay_recv_sem.at[region],
+            device_id=place(me + offsets[region] - hop),
+            device_id_type=MESH,
+        )
+
+    def forward_copy(region):
+        pos = place_of[region]
+        return pltpu.make_async_remote_copy(
+            src_ref=relay.at[pl.ds((pos - half) * ghost_rows, ghost_rows)],
+            dst_ref=ghosts.at[pl.ds(pos * ghost_rows, ghost_rows)],
+            send_sem=forward_sem.at[region],
+            recv_sem=recv_sem.at[region],
+            device_id=place(me + hop),
+            device_id_type=MESH,
+        )
+
+    def relayed(region):
+        if region not in upper:
+            return jnp.bool_(False)
+        return crosses(me + offsets[region], -offsets[region])
+
+    def direct(region):
+        return jnp.logical_and(exists(me + offsets[region]), jnp.logical_not(relayed(region)))
+
     for region in order:
-        @pl.when(exists(me + offsets[region]))
+        @pl.when(direct(region))
         def _():
             ghost_copy(region).start()
+
+        if region in upper:
+            @pl.when(relayed(region))
+            def _():
+                relay_copy(region).start()
 
     for pos, region in enumerate(order):
         @pl.when(jnp.logical_not(exists(me - offsets[region])))
@@ -246,8 +333,13 @@
         )
     for load in loads[5:]:
         load.wait()
-    viscous = viscous_ref[...].astype(jnp.float32).T.astype(jnp.bfloat16)
-    pressure = pressure_ref[...].astype(jnp.float32).T.astype(jnp.bfloat16)
+    both = jnp.concatenate(
+        [
+            viscous_ref[...].astype(jnp.float32).T.astype(jnp.bfloat16),
+            pressure_ref[...].astype(jnp.float32).T.astype(jnp.bfloat16),
+        ],
+        axis=0,
+    )
 
     receive(order[half:])
     dofs_t[:, middle:] = ghosts[split:].astype(jnp.float32).T.astype(jnp.bfloat16)
@@ -258,8 +350,8 @@
             dofs_t[:, middle:], rows_of(step, middle, columns), 1, 0
         )
         element_in = total.astype(jnp.bfloat16)
-        result = contract(viscous, element_in, 1, 0) * visc_ref[:, lanes]
-        result = result + contract(pressure, element_in, 1, 0)
+        applied = contract(both, element_in, 1, 0)
+        result = applied[:width] * visc_ref[:, lanes] + applied[width:]
         element_out[:, lanes] = result.astype(jnp.bfloat16)
 
     def back_copy(region):
@@ -284,10 +376,27 @@
             back_copy(region).start()
 
     back_out[:split] = scatter(owned, middle).astype(jnp.bfloat16)
+    late = jnp.int32(0)
+    for region in upper:
+        late = late + relayed(region).astype(jnp.int32)
+
+    @pl.when(late > 0)
+    def _():
+        pl.semaphore_wait(late_sem, late)
     for region in order[:half]:
         @pl.when(exists(me - offsets[region]))
         def _():
             back_copy(region).start()
+
+    @pl.when(any_cross(me + hop))
+    def _():
+        pl.semaphore_wait(ready_sem, 1)
+
+    for region in upper:
+        @pl.when(crosses(me + hop, -offsets[region]))
+        def _():
+            relay_copy(region).wait_recv()
+            forward_copy(region).start()
 
     out_ref[...] = scatter(0, owned)
 
@@ -301,9 +410,18 @@
         out_ref[...] += contract(mirror_table[:, low:high], back_in[low:high], 1, 0)
 
     for region in range(regions):
-        @pl.when(exists(me + offsets[region]))
+        @pl.when(direct(region))
         def _():
             ghost_copy(region).wait_send()
+
+        if region in upper:
+            @pl.when(relayed(region))
+            def _():
+                relay_copy(region).wait_send()
+
+            @pl.when(crosses(me + hop, -offsets[region]))
+            def _():
+                forward_copy(region).wait_send()
 
         @pl.when(exists(me - offsets[region]))
         def _():
@@ -353,8 +471,14 @@
             pltpu.VMEM((width, elems), bf16),
             pltpu.VMEM((regions * pad_rows, width), bf16),
             pltpu.VMEM((regions * ghost_rows, width), bf16),
+            pltpu.VMEM((regions // 2 * ghost_rows, width), bf16),
             pltpu.VMEM((regions * ghost_rows, width), bf16),
             pltpu.VMEM((regions * pad_rows, width), bf16),
+            pltpu.SemaphoreType.REGULAR,
+            pltpu.SemaphoreType.REGULAR,
+            pltpu.SemaphoreType.DMA((regions,)),
+            pltpu.SemaphoreType.DMA((regions,)),
+            pltpu.SemaphoreType.DMA((regions,)),
             pltpu.SemaphoreType.DMA((8,)),
             pltpu.SemaphoreType.DMA((regions,)),
             pltpu.SemaphoreType.DMA((regions,)),

time: 33.4 us -> 31.3 us (0.937)
  Pallas kernels: 31.6 us -> 29.7 us
    pallas_call x1, Pallas kernels: 31.6 us -> 29.7 us  [per_device(): pl.pallas_call(functools.partial(operator_kernel, n_curve, n_seg), out_sh...]
where the time goes in v4:
time: 31.3 us; the launch traced here: 31.1 us
  Pallas kernels  29.7 us (95%)
  local copies, waits for them, and re-layouts  0.71 us (2%)
  between operations  0.66 us (2%)
    pallas_call x1, Pallas kernels, per_device(): pl.pallas_call(functools.partial(operator_kernel, n_curve, n_seg), out_sh...  29.7 us
    unnamed x1, local copies, waits for them, and re-layouts  0.71 us

profile of v4, /device:TPU:56, one launch (start us, length us, event | category | flops | bytes accessed | tf_op | source)
XLA Modules:
  0.0 31.1 jit_solution(14984681712470681847)
XLA Ops:
  0.7 29.7 %shard_map.91 = f32[512,128]{1,0:T(8,128)S(1)} custom-call(s32[1]{0:T(128)S(6)} %copy.11.count_ref, bf16[512,128]{1,0:T(8,128)(2,1)} %solution_hbm.1, f32[1,4096]{1,0:T(1,128)} %bitcast.6, s32[4,4096]{1,0:T(4,128)} %bitcast.4, s32[4,4096]{1,0:T(4,128)} %bitcast.5, s32[4,192]{1,0:T(4,128)} %bitcast.7, s32[1,4]{1,0:T(1,128)} %live_hbm.1, ...), custom_call_target="tpu_custom_call" | custom-call | tf_op jit(solution)/shard_map/pallas_call | solution.py:452
  30.4 0.7 %copy.12 = f32[512,128]{1,0:T(8,128)} copy(f32[512,128]{1,0:T(8,128)S(1)} %shard_map.91) | data formatting | bytes 524288

commit v5 on v4

--- a/solution.py
+++ b/solution.py
@@ -278,6 +278,8 @@
     def owned_product(step):
         return contract(dofs_t[:, :owned], rows_of(step, 0, owned), 1, 0)
 
+    span = 64
+
     def build(step):
         for inner in range(per_step):
             group = step * per_step + inner
@@ -286,25 +288,41 @@
                 start = pl.multiple_of(start, lanes_of)
             lanes = pl.ds(start, lanes_of)
             live = (lax.broadcasted_iota(jnp.int32, (1, lanes_of), 1) + start) < count
-            index = [moved(index_ref[slot : slot + 1, lanes]) for slot in range(slots)]
-            raw = [
-                jnp.where(live, weight_ref[slot : slot + 1, lanes].astype(jnp.float32) * 0.125, 0.0)
-                for slot in range(slots)
-            ]
-            merged = []
+            shape = (sub, lanes_of)
+            blocks = []
+            patterns = []
             for slot in range(slots):
-                value = raw[slot]
+                index = index_ref[slot : slot + 1, lanes]
+                if slot:
+                    index = moved(index)
+                weight = weight_ref[slot : slot + 1, lanes].astype(jnp.float32) * 0.125
+                weight = jnp.broadcast_to(jnp.where(live, weight, 0.0), shape).astype(jnp.bfloat16)
+                rest = jnp.broadcast_to(jnp.bitwise_and(index, span - 1), shape).astype(jnp.int16) - row16
+                blocks.append(jnp.broadcast_to(jnp.right_shift(index, span.bit_length() - 1), shape).astype(jnp.int16))
+                patterns.append(
+                    [jnp.where(rest == jnp.int16(part * sub), weight, zero) for part in range(span // sub)]
+                )
+            summed = []
+            for slot in range(slots):
+                pattern = patterns[slot]
                 for other in range(slot):
-                    value = value + jnp.where(index[other] == index[slot], raw[other], 0.0)
-                merged.append(value)
-            shape = (sub, lanes_of)
-            ids = [jnp.broadcast_to(i, shape).astype(jnp.int16) - row16 for i in index]
-            wts = [jnp.broadcast_to(v, shape).astype(jnp.bfloat16) for v in merged]
-            for block in range(columns // sub):
-                value = zero
-                for slot in range(0 if block * sub < owned else 1, slots):
-                    value = jnp.where(ids[slot] == jnp.int16(block * sub), wts[slot], value)
-                table[group, block * sub : (block + 1) * sub, :] = value
+                    same = blocks[other] == blocks[slot]
+                    pattern = [
+                        mine + jnp.where(same, theirs, zero)
+                        for mine, theirs in zip(pattern, patterns[other])
+                    ]
+                summed.append(pattern)
+            for block in range(columns // span):
+                values = [zero] * (span // sub)
+                for slot in range(0 if block * span < owned else 1, slots):
+                    match = blocks[slot] == jnp.int16(block)
+                    values = [
+                        jnp.where(match, mine, value)
+                        for mine, value in zip(summed[slot], values)
+                    ]
+                for part in range(span // sub):
+                    row = block * span + part * sub
+                    table[group, row : row + sub, :] = values[part]
 
     def build_behind(step, carry):
         product = owned_product(step - 1)
@@ -344,12 +362,23 @@
     receive(order[half:])
     dofs_t[:, middle:] = ghosts[split:].astype(jnp.float32).T.astype(jnp.bfloat16)
 
-    for step in range(steps):
-        lanes = step_lanes(step)
-        total = gathered[:, lanes] + contract(
-            dofs_t[:, middle:], rows_of(step, middle, columns), 1, 0
-        )
-        element_in = total.astype(jnp.bfloat16)
+    width_of = 4
+    pieces = groups // width_of
+
+    def piece_lanes(piece):
+        return pl.ds(piece * width_of * lanes_of, width_of * lanes_of)
+
+    def upper_product(piece):
+        first = piece * width_of
+        rows = [table[first + inner, middle:columns, :] for inner in range(width_of)]
+        return contract(dofs_t[:, middle:], jnp.concatenate(rows, axis=1), 1, 0)
+
+    pending = [upper_product(piece) for piece in range(min(1, pieces))]
+    for piece in range(pieces):
+        if piece + 1 < pieces:
+            pending.append(upper_product(piece + 1))
+        lanes = piece_lanes(piece)
+        element_in = (gathered[:, lanes] + pending[piece]).astype(jnp.bfloat16)
         applied = contract(both, element_in, 1, 0)
         result = applied[:width] * visc_ref[:, lanes] + applied[width:]
         element_out[:, lanes] = result.astype(jnp.bfloat16)
@@ -369,8 +398,11 @@
         rows = jnp.concatenate([table[group, low:high, :] for group in range(groups)], axis=1)
         return contract(element_out[...], rows, 1, 1).T
 
-    back_out[split:] = scatter(middle, columns).astype(jnp.bfloat16)
-    for region in order[half:]:
+    for region in upper[::-1]:
+        start = place_of[region] * ghost_rows
+        stop = start + ghost_rows
+        back_out[start:stop] = scatter(owned + start, owned + stop).astype(jnp.bfloat16)
+
         @pl.when(exists(me - offsets[region]))
         def _():
             back_copy(region).start()

time: 31.3 us -> 30.2 us (0.965)
  Pallas kernels: 29.7 us -> 28.7 us
    pallas_call x1, Pallas kernels: 29.7 us -> 28.7 us  [per_device(): pl.pallas_call(functools.partial(operator_kernel, n_curve, n_seg), out_sh...]
where the time goes in v5:
time: 30.2 us; the launch traced here: 30.1 us
  Pallas kernels  28.7 us (95%)
  local copies, waits for them, and re-layouts  0.71 us (2%)
  between operations  0.66 us (2%)
    pallas_call x1, Pallas kernels, per_device(): pl.pallas_call(functools.partial(operator_kernel, n_curve, n_seg), out_sh...  28.7 us
    unnamed x1, local copies, waits for them, and re-layouts  0.71 us

profile of v5, /device:TPU:56, one launch (start us, length us, event | category | flops | bytes accessed | tf_op | source)
XLA Modules:
  0.0 30.1 jit_solution(17483423510478958068)
XLA Ops:
  0.7 28.7 %shard_map.91 = f32[512,128]{1,0:T(8,128)S(1)} custom-call(s32[1]{0:T(128)S(6)} %copy.11.count_ref, bf16[512,128]{1,0:T(8,128)(2,1)} %solution_hbm.1, f32[1,4096]{1,0:T(1,128)} %bitcast.6, s32[4,4096]{1,0:T(4,128)} %bitcast.4, s32[4,4096]{1,0:T(4,128)} %bitcast.5, s32[4,192]{1,0:T(4,128)} %bitcast.7, s32[1,4]{1,0:T(1,128)} %live_hbm.1, ...), custom_call_target="tpu_custom_call" | custom-call | tf_op jit(solution)/shard_map/pallas_call | solution.py:484
  29.4 0.7 %copy.12 = f32[512,128]{1,0:T(8,128)} copy(f32[512,128]{1,0:T(8,128)S(1)} %shard_map.91) | data formatting | bytes 524288

commit v6 on v5

--- a/solution.py
+++ b/solution.py
@@ -8,6 +8,7 @@
 from jax.sharding import PartitionSpec as P
 
 LANES = 128
+PIECE = 192
 ROW = 12
 MESH = pl.DeviceIdType.MESH
 
@@ -362,7 +363,7 @@
     receive(order[half:])
     dofs_t[:, middle:] = ghosts[split:].astype(jnp.float32).T.astype(jnp.bfloat16)
 
-    width_of = 4
+    width_of = per_step
     pieces = groups // width_of
 
     def piece_lanes(piece):
@@ -381,7 +382,7 @@
         element_in = (gathered[:, lanes] + pending[piece]).astype(jnp.bfloat16)
         applied = contract(both, element_in, 1, 0)
         result = applied[:width] * visc_ref[:, lanes] + applied[width:]
-        element_out[:, lanes] = result.astype(jnp.bfloat16)
+        element_out[lanes, :] = result.T.astype(jnp.bfloat16)
 
     def back_copy(region):
         pos = place_of[region]
@@ -396,7 +397,7 @@
 
     def scatter(low, high):
         rows = jnp.concatenate([table[group, low:high, :] for group in range(groups)], axis=1)
-        return contract(element_out[...], rows, 1, 1).T
+        return contract(rows, element_out[...], 1, 0)
 
     for region in upper[::-1]:
         start = place_of[region] * ghost_rows
@@ -407,7 +408,6 @@
         def _():
             back_copy(region).start()
 
-    back_out[:split] = scatter(owned, middle).astype(jnp.bfloat16)
     late = jnp.int32(0)
     for region in upper:
         late = late + relayed(region).astype(jnp.int32)
@@ -416,6 +416,10 @@
     def _():
         pl.semaphore_wait(late_sem, late)
     for region in order[:half]:
+        start = place_of[region] * ghost_rows
+        stop = start + ghost_rows
+        back_out[start:stop] = scatter(owned + start, owned + stop).astype(jnp.bfloat16)
+
         @pl.when(exists(me - offsets[region]))
         def _():
             back_copy(region).start()
@@ -430,7 +434,9 @@
             relay_copy(region).wait_recv()
             forward_copy(region).start()
 
-    out_ref[...] = scatter(0, owned)
+    for start in range(0, owned, PIECE):
+        stop = min(start + PIECE, owned)
+        out_ref[start:stop] = scatter(start, stop)
 
     for chosen, low in ((order[:half], 0), (order[half:], half * pad_rows)):
         for region in chosen:
@@ -500,7 +506,7 @@
             pltpu.VMEM((owned, regions * pad_rows), bf16),
             pltpu.VMEM((width, columns), bf16),
             pltpu.VMEM((width, elems), f32),
-            pltpu.VMEM((width, elems), bf16),
+            pltpu.VMEM((elems, width), bf16),
             pltpu.VMEM((regions * pad_rows, width), bf16),
             pltpu.VMEM((regions * ghost_rows, width), bf16),
             pltpu.VMEM((regions // 2 * ghost_rows, width), bf16),

time: 30.2 us -> 29.7 us (0.983)
  Pallas kernels: 28.7 us -> 28.1 us
    pallas_call x1, Pallas kernels: 28.7 us -> 28.1 us  [per_device(): pl.pallas_call(functools.partial(operator_kernel, n_curve, n_seg), out_sh...]
where the time goes in v6:
time: 29.7 us; the launch traced here: 29.5 us
  Pallas kernels  28.1 us (95%)
  local copies, waits for them, and re-layouts  0.71 us (2%)
  between operations  0.66 us (2%)
    pallas_call x1, Pallas kernels, per_device(): pl.pallas_call(functools.partial(operator_kernel, n_curve, n_seg), out_sh...  28.1 us
    unnamed x1, local copies, waits for them, and re-layouts  0.71 us

profile of v6, /device:TPU:56, one launch (start us, length us, event | category | flops | bytes accessed | tf_op | source)
XLA Modules:
  0.0 29.5 jit_solution(1021567592897905)
XLA Ops:
  0.7 28.1 %shard_map.91 = f32[512,128]{1,0:T(8,128)S(1)} custom-call(s32[1]{0:T(128)S(6)} %copy.11.count_ref, bf16[512,128]{1,0:T(8,128)(2,1)} %solution_hbm.1, f32[1,4096]{1,0:T(1,128)} %bitcast.6, s32[4,4096]{1,0:T(4,128)} %bitcast.4, s32[4,4096]{1,0:T(4,128)} %bitcast.5, s32[4,192]{1,0:T(4,128)} %bitcast.7, s32[1,4]{1,0:T(1,128)} %live_hbm.1, ...), custom_call_target="tpu_custom_call" | custom-call | tf_op jit(solution)/shard_map/pallas_call | solution.py:490
  28.8 0.7 %copy.12 = f32[512,128]{1,0:T(8,128)} copy(f32[512,128]{1,0:T(8,128)S(1)} %shard_map.91) | data formatting | bytes 524288

commit v7 on v6

--- a/solution.py
+++ b/solution.py
@@ -101,29 +101,6 @@
     def any_cross(device):
         return crosses(device, reach)
 
-    barrier = pltpu.get_barrier_semaphore()
-
-    def greet(device):
-        pl.semaphore_signal(barrier, inc=1, device_id=place(device), device_id_type=MESH)
-
-    for offset in offsets:
-        wanted = exists(me + offset)
-        if offset > 0:
-            wanted = jnp.logical_and(wanted, jnp.logical_not(crosses(me, offset)))
-
-        @pl.when(wanted)
-        def _():
-            greet(me + offset)
-
-    @pl.when(any_cross(me + hop))
-    def _():
-        greet(me + hop)
-
-    for region in upper:
-        @pl.when(crosses(me + hop, -offsets[region]))
-        def _():
-            greet(me + hop - offsets[region])
-
     pairs = [
         (mirror_hbm, mirror_ref),
         (live_hbm, live_ref),
@@ -140,6 +117,29 @@
     ]
     for load in loads:
         load.start()
+
+    barrier = pltpu.get_barrier_semaphore()
+
+    def greet(device):
+        pl.semaphore_signal(barrier, inc=1, device_id=place(device), device_id_type=MESH)
+
+    for offset in offsets:
+        wanted = exists(me + offset)
+        if offset > 0:
+            wanted = jnp.logical_and(wanted, jnp.logical_not(crosses(me, offset)))
+
+        @pl.when(wanted)
+        def _():
+            greet(me + offset)
+
+    @pl.when(any_cross(me + hop))
+    def _():
+        greet(me + hop)
+
+    for region in upper:
+        @pl.when(crosses(me + hop, -offsets[region]))
+        def _():
+            greet(me + hop - offsets[region])
 
     sub = 16
     row16 = lax.broadcasted_iota(jnp.int32, (sub, lanes_of), 0).astype(jnp.int16)
@@ -163,10 +163,6 @@
                 hit = jnp.where(picks == jnp.int16(block * sub), one, zero)
                 start = pos * pad_rows + first
                 mirror_table[block * sub : (block + 1) * sub, start : start + LANES] = hit
-    dofs_t[:, :owned] = solution_ref[...].astype(jnp.float32).T.astype(jnp.bfloat16)
-    listed = contract(dofs_t[:, :owned], mirror_table[...], 1, 0)
-    outgoing[...] = listed.T.astype(jnp.bfloat16)
-
     peers = any_cross(me).astype(jnp.int32)
     for offset in offsets:
         peers = peers + exists(me + offset).astype(jnp.int32)
@@ -181,6 +177,10 @@
         def _():
             target = place(me - offsets[region])
             pl.semaphore_signal(late_sem, inc=1, device_id=target, device_id_type=MESH)
+
+    dofs_t[:, :owned] = solution_ref[...].astype(jnp.float32).T.astype(jnp.bfloat16)
+    listed = contract(dofs_t[:, :owned], mirror_table[...], 1, 0)
+    outgoing[...] = listed.T.astype(jnp.bfloat16)
 
     def ghost_copy(region):
         pos = place_of[region]
@@ -445,7 +445,11 @@
                 back_copy(region).wait_recv()
 
         high = low + half * pad_rows
-        out_ref[...] += contract(mirror_table[:, low:high], back_in[low:high], 1, 0)
+        for start in range(0, owned, PIECE):
+            stop = min(start + PIECE, owned)
+            out_ref[start:stop] += contract(
+                mirror_table[start:stop, low:high], back_in[low:high], 1, 0
+            )
 
     for region in range(regions):
         @pl.when(direct(region))

time: 29.7 us -> 29.1 us (0.980)
  Pallas kernels: 28.1 us -> 27.6 us
    pallas_call x1, Pallas kernels: 28.1 us -> 27.6 us  [per_device(): pl.pallas_call(functools.partial(operator_kernel, n_curve, n_seg), out_sh...]
where the time goes in v7:
time: 29.1 us; the launch traced here: 28.9 us
  Pallas kernels  27.6 us (95%)
  local copies, waits for them, and re-layouts  0.71 us (2%)
  between operations  0.66 us (2%)
    pallas_call x1, Pallas kernels, per_device(): pl.pallas_call(functools.partial(operator_kernel, n_curve, n_seg), out_sh...  27.6 us
    unnamed x1, local copies, waits for them, and re-layouts  0.71 us

profile of v7, /device:TPU:56, one launch (start us, length us, event | category | flops | bytes accessed | tf_op | source)
XLA Modules:
  0.0 28.9 jit_solution(17792029476716703946)
XLA Ops:
  0.7 27.6 %shard_map.91 = f32[512,128]{1,0:T(8,128)S(1)} custom-call(s32[1]{0:T(128)S(6)} %copy.11.count_ref, bf16[512,128]{1,0:T(8,128)(2,1)} %solution_hbm.1, f32[1,4096]{1,0:T(1,128)} %bitcast.6, s32[4,4096]{1,0:T(4,128)} %bitcast.4, s32[4,4096]{1,0:T(4,128)} %bitcast.5, s32[4,192]{1,0:T(4,128)} %bitcast.7, s32[1,4]{1,0:T(1,128)} %live_hbm.1, ...), custom_call_target="tpu_custom_call" | custom-call | tf_op jit(solution)/shard_map/pallas_call | solution.py:494
  28.2 0.7 %copy.12 = f32[512,128]{1,0:T(8,128)} copy(f32[512,128]{1,0:T(8,128)S(1)} %shard_map.91) | data formatting | bytes 524288
